TPU v7x, 16 devices: a 4x2x1 block of a 4x4x8 slice. The times are simulated.
16 devices in a mesh: dp: 2 (over y, z), tp: 8 (over x, core).
Axes of the slice: x: 4, y: 2, z: 1, core: 2. Of those that a mesh axis runs over, the one named last changes fastest.
The devices are a block of a 4x4x8 slice.
Arguments:
- x: bfloat16 [512, 4096], P('dp'), parts along dimension 0
- lengths: int32 [512], P('dp'), parts along dimension 0
- k_cache: bfloat16 [2, 512, 128, 8, 128], P(None, 'dp', None, 'tp'), parts along dimension 1
- v_cache: bfloat16 [2, 512, 128, 8, 128], P(None, 'dp', None, 'tp'), parts along dimension 1
- attn_norm: float32 [2, 4096], replicated
- mlp_norm: float32 [2, 4096], replicated
- w_q: bfloat16 [2, 4096, 4096], P(None, None, 'tp')
- w_k: bfloat16 [2, 4096, 1024], P(None, None, 'tp')
- w_v: bfloat16 [2, 4096, 1024], P(None, None, 'tp')
- w_o: bfloat16 [2, 4096, 4096], P(None, 'tp')
- w_gate: bfloat16 [2, 4096, 14336], P(None, None, 'tp')
- w_up: bfloat16 [2, 4096, 14336], P(None, None, 'tp')
- w_down: bfloat16 [2, 14336, 4096], P(None, 'tp')
Outputs:
- output: bfloat16 [512, 4096], P('dp'), parts along dimension 0
There are 2 independent parts. A program takes and returns all parts, laid end to end along the dimension named above; an argument that names none is the same for every part.
All inputs are finite; a program needn't handle non-finite values.
Results may differ from a plain program's by a relative error of at most 0.02.
Values are sent between devices in bfloat16 or wider.
A program may use at most 768 MiB of HBM per device.

v0:
```python
import functools

import jax
import jax.numpy as jnp
from jax import lax
from jax.experimental import pallas as pl
from jax.experimental.pallas import tpu as pltpu
from jax.sharding import PartitionSpec as P

NORM_EPS = 1e-5
ROPE_BASE = 10000.0
BF = jnp.bfloat16
F32 = jnp.float32
CHUNKS = 2
TOK = 16
NKV = 4
GRP = 4
TILE = 256
COPIES = ("part", "far", "near", "relay", "ssq", "g_fwd", "g_bwd", "g_far", "p_own", "p_bwd", "p_fwd", "p_far")


def dot(a, b):
    return jnp.dot(a, b, preferred_element_type=F32)


def kernel(
    x, cos, sin, nrow, kc, vc, an, mn, wq, wk, wv, wo, wg, wu, wd, out,
    wa, wb, kbuf, vbuf, cbuf, pbuf, dbuf, xs, ys, zs, xr, yr, zr, qsum, rsum, hres, act, qs, kx, vx, osc, obf,
    sem_a, sem_b, sem_k, sem_v, sem_x, ssem, rsem,
):
    n_layers = wq.shape[0]
    batch, width = x.shape
    chunk = batch // CHUNKS
    half = width // 2
    head = kc.shape[3]
    heads = wq.shape[2] // head
    n_ff = wg.shape[2] // TILE
    n_o = wo.shape[1] // TILE
    n_q = wq.shape[2] // TILE
    n_tp = lax.axis_size("tp")
    chips = n_tp // 2
    rows = chunk // chips
    steps = chunk // TOK
    scale = head ** -0.5

    me = lax.axis_index("tp")
    core = lax.rem(me, 2)
    chip = lax.div(me, 2)
    sign = 1 - 2 * core
    fwd_chip = lax.rem(chip + sign + chips, chips)
    bwd_chip = lax.rem(chip - sign + chips, chips)
    far_chip = lax.rem(chip + 2, chips)
    fwd, bwd = fwd_chip * 2 + core, bwd_chip * 2 + core
    peer = chip * 2 + 1 - core

    def rows_of(c):
        return pl.ds(pl.multiple_of(c * rows, rows), rows)

    own_cols = pl.ds(pl.multiple_of(core * half, half), half)
    peer_cols = pl.ds(pl.multiple_of((1 - core) * half, half), half)

    def load_a(layer, t):
        src = (wg, wu)[t % 2]
        return [pltpu.make_async_copy(src.at[layer, :, pl.ds((t // 2) * TILE, TILE)], wa.at[t], sem_a.at[t])]

    def load_q(layer, t):
        return [pltpu.make_async_copy(wq.at[layer, :, pl.ds(t * TILE, TILE)], wa.at[t], sem_a.at[t])]

    def load_kv(layer):
        t = n_q
        return [
            pltpu.make_async_copy(wk.at[layer], wa.at[t, :, pl.ds(0, head)], sem_a.at[t]),
            pltpu.make_async_copy(wv.at[layer], wa.at[t, :, pl.ds(head, head)], sem_k.at[NKV]),
        ]

    def load_o(layer, t):
        return [pltpu.make_async_copy(wo.at[layer, pl.ds(t * TILE, TILE), :], wb.at[t], sem_b.at[t])]

    def load_d(layer, t):
        return [pltpu.make_async_copy(wd.at[layer, pl.ds(t * TILE, TILE), :], wb.at[t], sem_b.at[t])]

    def begin(copies, priority=1):
        for c in copies:
            c.start(priority=priority)

    def finish(copies):
        for c in copies:
            c.wait()

    def load_cache(g):
        layer = g // (CHUNKS * steps)
        tok = pl.multiple_of(lax.rem(g, CHUNKS * steps) * TOK, TOK)
        slot = lax.rem(g, NKV)
        return [
            pltpu.make_async_copy(kc.at[layer, pl.ds(tok, TOK)], kbuf.at[slot], sem_k.at[slot]),
            pltpu.make_async_copy(vc.at[layer, pl.ds(tok, TOK)], vbuf.at[slot], sem_v.at[slot]),
        ]

    def load_x(ch):
        return [
            pltpu.make_async_copy(x.at[pl.ds(ch * chunk, chunk), :], pbuf.at[ch], sem_x.at[ch, 0]),
            pltpu.make_async_copy(
                x.at[pl.ds(pl.multiple_of(ch * chunk + chip * rows, rows), rows), own_cols], hres.at[ch], sem_x.at[ch, 1]
            ),
        ]

    n_attn = n_q + 1

    begin(load_x(0), 0)
    for t in range(n_q):
        begin(load_q(0, t), 0)
    begin(load_kv(0), 0)
    for g in range(NKV):
        begin(load_cache(jnp.int32(g)), 0)
    begin(load_x(1), 0)
    for t in range(n_o):
        begin(load_o(0, t))
    for t in range(n_attn, 2 * n_ff):
        begin(load_a(0, t))
    for t in range(n_o, n_ff):
        begin(load_d(0, t))

    barrier = pltpu.get_barrier_semaphore()
    for other in (peer, fwd, bwd):
        pl.semaphore_signal(barrier, inc=1, device_id={"tp": other}, device_id_type=pl.DeviceIdType.MESH)
    pl.semaphore_wait(barrier, 3)

    def first_norm(ch):
        finish(load_x(ch))

        def body(i, _):
            r = pl.ds(pl.multiple_of(i * 16, 16), 16)
            h = pbuf[ch, r, :].astype(F32)
            inv = lax.rsqrt(jnp.mean(h * h, axis=-1, keepdims=True) + NORM_EPS)
            cbuf[ch, r, :] = (h * inv * an[0:1, :]).astype(BF)
            return 0

        lax.fori_loop(0, chunk // 16, body, 0)

    def remote(ch, name, src, dst, target):
        i = COPIES.index(name)
        return pltpu.make_async_remote_copy(
            src_ref=src,
            dst_ref=dst,
            send_sem=ssem.at[ch, i],
            recv_sem=rsem.at[ch, i],
            device_id={"tp": target},
            device_id_type=pl.DeviceIdType.MESH,
        )

    def block(ch, c, cols):
        return cbuf.at[ch, rows_of(c), cols]

    def copies_of(ch):
        d = {
            "part": remote(ch, "part", pbuf.at[ch, :, peer_cols], dbuf.at[ch], peer),
            "far": remote(ch, "far", xs.at[ch], xr.at[ch], fwd),
            "near": remote(ch, "near", ys.at[ch], yr.at[ch], bwd),
            "relay": remote(ch, "relay", zs.at[ch], zr.at[ch], fwd),
            "ssq": remote(ch, "ssq", qsum.at[ch], rsum.at[ch], peer),
        }
        for name, c, target in (
            ("g_fwd", chip, fwd), ("g_bwd", chip, bwd), ("g_far", bwd_chip, fwd),
            ("p_own", chip, peer), ("p_bwd", bwd_chip, peer), ("p_fwd", fwd_chip, peer), ("p_far", far_chip, peer),
        ):
            d[name] = remote(ch, name, block(ch, c, own_cols), block(ch, c, own_cols), target)
        return d

    def pair(ch, c):
        return pbuf[ch, rows_of(c), own_cols].astype(F32) + dbuf[ch, rows_of(c), :].astype(F32)

    def exchange(ch, gain, last):
        d = copies_of(ch)
        d["part"].wait_recv()
        xs[ch] = pair(ch, far_chip)
        d["far"].start()
        ys[ch] = pair(ch, bwd_chip)
        d["near"].start()
        yield
        d["far"].wait_recv()
        zs[ch] = xr[ch] + pair(ch, fwd_chip)
        d["relay"].start()
        yield
        d["near"].wait_recv()
        d["relay"].wait_recv()
        h = (hres[ch].astype(F32) + (pair(ch, chip) + yr[ch] + zr[ch])).astype(BF)
        if last:
            cbuf[ch, rows_of(chip), own_cols] = h
        else:
            hres[ch] = h
            hf = h.astype(F32)
            qsum[ch] = jnp.broadcast_to(jnp.sum(hf * hf, axis=-1, keepdims=True), (rows, 128))
            d["ssq"].start()
            yield
            d["ssq"].wait_recv()
            total = (qsum[ch] + rsum[ch])[:, 0:1]
            inv = lax.rsqrt(total * (1.0 / width) + NORM_EPS)
            cbuf[ch, rows_of(chip), own_cols] = (hres[ch].astype(F32) * inv * gain[:, own_cols]).astype(BF)
        for name in ("g_fwd", "g_bwd", "p_own"):
            d[name].start()
        yield
        d["g_fwd"].wait_recv()
        d["g_far"].start()
        d["p_bwd"].start()
        d["g_bwd"].wait_recv()
        d["p_fwd"].start()
        yield
        d["g_far"].wait_recv()
        d["p_far"].start()
        yield
        for name in ("p_own", "p_bwd", "p_fwd", "p_far"):
            d[name].wait_recv()
        for name in COPIES:
            if not (last and name == "ssq"):
                d[name].wait_send()

    n_col = 512
    per_half = half // n_col

    def partial_cols(ch, product, lo, hi):
        def body(n, _):
            col = lax.rem((1 - core) * half + n * n_col, width)
            cols = pl.ds(pl.multiple_of(col, n_col), n_col)
            pbuf[ch, :, cols] = product(cols).astype(BF)
            return 0

        lax.fori_loop(lo, hi, body, 0)

    def attention(layer, ch):
        tok = pl.ds(ch * chunk, chunk)
        ct, st = cos[tok, :], sin[tok, :]

        def rope(v):
            return (v * ct + pltpu.roll(v, head // 2, 1) * st).astype(BF).astype(F32)

        for t in range(n_q):
            if ch == 0:
                finish(load_q(layer, t))
            q2 = dot(cbuf[ch], wa[t])
            for i in range(TILE // head):
                h = t * (TILE // head) + i
                qs[pl.ds(h, chunk, stride=heads), :] = rope(q2[:, i * head:(i + 1) * head])
        if ch == 0:
            finish(load_kv(layer))
        kv = dot(cbuf[ch], wa[n_q])
        k_new = rope(kv[:, :head])
        v_new = kv[:, head:].astype(BF).astype(F32)
        for h in range(heads):
            kx[pl.ds(h, chunk, stride=heads), :] = k_new
            vx[pl.ds(h, chunk, stride=heads), :] = v_new
        if ch == CHUNKS - 1:
            for t in range(n_attn):
                begin(load_a(layer, t))
        yield

        def step(i, _):
            g = (layer * CHUNKS + ch) * steps + i
            slot = lax.rem(g, NKV)
            finish(load_cache(g))
            qrows = GRP * heads
            row_tok = lax.broadcasted_iota(jnp.int32, (qrows, head), 0) // heads
            pos = lax.broadcasted_iota(jnp.int32, (qrows, head), 1)
            for j in range(TOK // GRP):
                r = pl.ds(pl.multiple_of((i * (TOK // GRP) + j) * qrows, qrows), qrows)
                rn = pl.ds(pl.multiple_of(ch * chunk * heads + (i * (TOK // GRP) + j) * qrows, qrows), qrows)
                q = qs[r, :]
                kg = kbuf[slot, pl.ds(j * GRP, GRP)].reshape(GRP * kbuf.shape[2], head)
                vg = vbuf[slot, pl.ds(j * GRP, GRP)].reshape(GRP * kbuf.shape[2], head)
                lg = lax.dot_general(q.astype(BF), kg, (((1,), (1,)), ((), ())), preferred_element_type=F32) * scale
                n = nrow[rn, :]
                parts = [
                    jnp.where(pos < jnp.where(row_tok == b, n, 0), lg[:, b * head:(b + 1) * head], -1e30)
                    for b in range(GRP)
                ]
                l_new = jnp.sum(q * kx[r, :], axis=-1, keepdims=True) * scale
                top = functools.reduce(jnp.maximum, parts)
                m = jnp.maximum(jnp.max(top, axis=-1, keepdims=True), l_new)
                ps = [jnp.exp(b - m) for b in parts]
                p_new = jnp.exp(l_new - m)
                total = jnp.sum(functools.reduce(jnp.add, ps), axis=-1, keepdims=True) + p_new
                o = dot(jnp.concatenate(ps, axis=1).astype(BF), vg)
                o = o + p_new.astype(BF).astype(F32) * vx[r, :]
                osc[r, :] = o / total

            @pl.when(g + NKV < n_layers * CHUNKS * steps)
            def _():
                begin(load_cache(g + NKV), 0)

            return 0

        for lo, hi in ((0, steps // 2), (steps // 2, steps)):
            lax.fori_loop(lo, hi, step, 0)
            yield

        for h in range(heads):
            obf[:, h * head:(h + 1) * head] = osc[pl.ds(h, chunk, stride=heads), :].astype(BF)
        if ch == 0:
            for t in range(n_o):
                finish(load_o(layer, t))

        def product(cols):
            return functools.reduce(
                jnp.add, [dot(obf[:, t * TILE:(t + 1) * TILE], wb[t, :, cols]) for t in range(n_o)]
            )

        partial_cols(ch, product, 0, per_half)
        copies_of(ch)["part"].start()
        yield
        partial_cols(ch, product, per_half, 2 * per_half)
        if ch == CHUNKS - 1:
            for t in range(n_o):
                begin(load_d(layer, t))

    def mlp(layer, ch):
        more = ch == CHUNKS - 1 and layer + 1 < n_layers

        for j in range(n_ff):
            if ch == 0:
                finish(load_a(layer, 2 * j))
                finish(load_a(layer, 2 * j + 1))
            gate = dot(cbuf[ch], wa[2 * j])
            up = dot(cbuf[ch], wa[2 * j + 1])
            act[j] = (gate * (1.0 / (1.0 + jnp.exp(-gate))) * up).astype(BF)
            if more:
                for t in (2 * j, 2 * j + 1):
                    if t < n_q:
                        begin(load_q(layer + 1, t))
                    elif t == n_q:
                        begin(load_kv(layer + 1))
                    else:
                        begin(load_a(layer + 1, t))
            yield
        if ch == 0:
            for t in range(n_ff):
                finish(load_d(layer, t))

        def product(cols):
            return functools.reduce(jnp.add, [dot(act[t], wb[t, :, cols]) for t in range(n_ff)])

        partial_cols(ch, product, 0, per_half)
        copies_of(ch)["part"].start()
        yield
        partial_cols(ch, product, per_half, 2 * per_half)
        if more:
            for t in range(n_ff):
                begin(load_o(layer + 1, t) if t < n_o else load_d(layer + 1, t))

    def drain(gen):
        if gen is not None:
            for _ in gen:
                pass

    stages = [(kind, layer, ch) for layer in range(n_layers) for kind in ("attn", "mlp") for ch in range(CHUNKS)]
    pending = {}
    for kind, layer, ch in stages:
        other = pending.get(1 - ch)
        drain(pending.pop(ch, None))
        if kind == "attn" and layer == 0:
            first_norm(ch)
        for _ in (attention if kind == "attn" else mlp)(layer, ch):
            if other is not None:
                next(other, None)
        last = kind == "mlp" and layer + 1 == n_layers
        nxt = min(layer + 1, n_layers - 1)
        gain = mn.at[layer:layer + 1] if kind == "attn" else an.at[nxt:nxt + 1]
        pending[ch] = exchange(ch, gain, last)
        next(pending[ch])
    outs = []
    for ch in range(CHUNKS):
        drain(pending.pop(ch))
        outs.append(pltpu.make_async_copy(cbuf.at[ch], out.at[pl.ds(ch * chunk, chunk), :], sem_x.at[ch, 0]))
        outs[-1].start()
    for c in outs:
        c.wait()


def solution(mesh):
    cache_spec = P(None, "dp", None, "tp", None)
    col_spec = P(None, None, "tp")
    row_spec = P(None, "tp", None)
    in_specs = (P("dp", None), P("dp"), cache_spec, cache_spec, P(), P(), col_spec, col_spec, col_spec, row_spec, col_spec, col_spec, row_spec)

    def local_layers(x, lengths, k_cache, v_cache, attn_norm, mlp_norm, w_q, w_k, w_v, w_o, w_gate, w_up, w_down):
        batch, width = x.shape
        layers, _, seq, _, head = k_cache.shape
        heads = w_q.shape[2] // head
        inner = w_o.shape[1]
        ff = w_gate.shape[2]
        chips = mesh.shape["tp"] // 2
        chunk = batch // CHUNKS
        rows = chunk // chips
        half = width // 2

        inv_freq = ROPE_BASE ** (-jnp.arange(0, head, 2).astype(F32) / head)
        angles = lengths.astype(F32)[:, None] * inv_freq[None, :]
        ct, st = jnp.cos(angles), jnp.sin(angles)
        cos = jnp.concatenate([ct, ct], axis=1)
        sin = jnp.concatenate([-st, st], axis=1)
        nrow = jnp.broadcast_to(lengths[:, None, None], (batch, heads, head)).reshape(batch * heads, head)

        vmem = pl.BlockSpec(memory_space=pltpu.VMEM)
        hbm = pl.BlockSpec(memory_space=pl.ANY)
        n_wa = 2 * (ff // TILE)
        n_wb = ff // TILE
        f32_half = pltpu.VMEM((CHUNKS, rows, half), F32)
        return pl.pallas_call(
            kernel,
            out_shape=jax.ShapeDtypeStruct((batch, width), BF),
            in_specs=[hbm, vmem, vmem, vmem, hbm, hbm, vmem, vmem] + [hbm] * 7,
            out_specs=hbm,
            scratch_shapes=[
                pltpu.VMEM((n_wa, width, TILE), BF),
                pltpu.VMEM((n_wb, TILE, width), BF),
                pltpu.VMEM((NKV, TOK, seq, head), BF),
                pltpu.VMEM((NKV, TOK, seq, head), BF),
                pltpu.VMEM((CHUNKS, chunk, width), BF),
                pltpu.VMEM((CHUNKS, chunk, width), BF),
                pltpu.VMEM((CHUNKS, chunk, half), BF),
                f32_half, f32_half, f32_half, f32_half, f32_half, f32_half,
                pltpu.VMEM((CHUNKS, rows, 128), F32),
                pltpu.VMEM((CHUNKS, rows, 128), F32),
                pltpu.VMEM((CHUNKS, rows, half), BF),
                pltpu.VMEM((n_wb, chunk, TILE), BF),
                pltpu.VMEM((chunk * heads, head), F32),
                pltpu.VMEM((chunk * heads, head), F32),
                pltpu.VMEM((chunk * heads, head), F32),
                pltpu.VMEM((chunk * heads, head), F32),
                pltpu.VMEM((chunk, inner), BF),
                pltpu.SemaphoreType.DMA((n_wa,)),
                pltpu.SemaphoreType.DMA((n_wb,)),
                pltpu.SemaphoreType.DMA((NKV + 1,)),
                pltpu.SemaphoreType.DMA((NKV,)),
                pltpu.SemaphoreType.DMA((CHUNKS, 2)),
                pltpu.SemaphoreType.DMA((CHUNKS, len(COPIES))),
                pltpu.SemaphoreType.DMA((CHUNKS, len(COPIES))),
            ],
            compiler_params=pltpu.CompilerParams(
                collective_id=0, has_side_effects=True, vmem_limit_bytes=67043328
            ),
            name="decoder",
        )(
            x, cos, sin, nrow,
            k_cache.reshape(layers, batch, seq, head), v_cache.reshape(layers, batch, seq, head),
            attn_norm, mlp_norm, w_q, w_k, w_v, w_o, w_gate, w_up, w_down,
        )

    return jax.shard_map(local_layers, mesh=mesh, in_specs=in_specs, out_specs=P("dp", None), check_vma=False)
```

profile of v0, /device:TPU:113, one launch (start us, length us, event | category | flops | bytes accessed | tf_op | source)
XLA Modules:
  0.0 239.7 jit_solution(17038656946049197673)
XLA Ops:
  0.0 0.7 convert_element_type.10
  0.7 0.8 broadcast_in_dim.12
  1.5 0.1 broadcast_in_dim.13
  1.6 0.5 fusion
  2.1 0.9 pad_maximum_fusion
  3.0 1.0 broadcast_in_dim.14.nrow
  4.0 232.5 %decoder.1 = bf16[256,4096]{1,0:T(8,128)(2,1)} custom-call(bf16[256,4096]{1,0:T(8,128)(2,1)} %x.1, f32[256,128]{1,0:T(8,128)} %get-tuple-element.8.cos, f32[256,128]{1,0:T(8,128)} %get-tuple-element.9.sin, s32[1024,128]{1,0:T(8,128)} %broadcast_in_dim.14.nrow, bf16[2,256,128,128]{3,2,1,0:T(8,128)(2,1)} %bitcast.2, bf16[2,256,128,128]{3,2,1,0:T(8,128)(2,1)} %bitcast.3, ...), custom_call_target="tpu_custom_call" | custom-call | tf_op jit(solution)/shard_map/decoder/pallas_call | solution.py:406
  236.5 3.1 %copy.15 = bf16[256,4096]{1,0:T(8,128)(2,1)} copy(bf16[256,4096]{1,0:T(8,128)(2,1)} %decoder.1) | data formatting | bytes 4194304
  (1 shorter events, 0.0 us)
where the time goes:
time: 240 us
  Pallas kernels  233 us (97%)
  local copies, waits for them, and re-layouts  5.01 us (2%)
    pallas_call x1, Pallas kernels, local_layers(): pl.pallas_call(kernel, out_shape=jax.ShapeDtypeStruct((batch, width), BF)...  233 us

commit v1 on v0

v1 whole, which is shorter than its diff:
```python
import functools

import jax
import jax.numpy as jnp
from jax import lax
from jax.experimental import pallas as pl
from jax.experimental.pallas import tpu as pltpu
from jax.sharding import PartitionSpec as P

NORM_EPS = 1e-5
ROPE_BASE = 10000.0
BF = jnp.bfloat16
F32 = jnp.float32
CHUNKS = 2
TOK = 16
NKV = 4
GRP = 4
TILE = 256
NP = 4
LAG = 2
ONCE = ("near", "g_fwd", "g_bwd", "g_far", "p_own", "p_bwd", "p_fwd", "p_far")
COPIES = ONCE + tuple(f"{k}{p}" for k in ("part", "far", "relay") for p in range(NP))


def dot(a, b):
    return jnp.dot(a, b, preferred_element_type=F32)


def kernel(
    x, cos, sin, nrow, kc, vc, an, mn, wq, wk, wv, wo, wg, wu, wd, out,
    wa, wb, kbuf, vbuf, cbuf, pbuf, dbuf, xs, ys, zs, xr, yr, zr, hres, act, qs, kx, vx, osc, obf,
    sem_a, sem_b, sem_k, sem_v, sem_x, ssem, rsem,
):
    n_layers = wq.shape[0]
    width = x.shape[-1]
    n_tp = lax.axis_size("tp")
    chunk = n_tp * x.shape[3]
    head = kc.shape[3]
    heads = wq.shape[2] // head
    n_ff = wg.shape[2] // TILE
    n_o = wo.shape[1] // TILE
    n_q = wq.shape[2] // TILE
    chips = n_tp // 2
    rows = chunk // n_tp
    piece = width // NP
    steps = chunk // TOK
    scale = head ** -0.5

    me = lax.axis_index("tp")
    core = lax.rem(me, 2)
    chip = lax.div(me, 2)
    sign = 1 - 2 * core
    fwd_chip = lax.rem(chip + sign + chips, chips)
    bwd_chip = lax.rem(chip - sign + chips, chips)
    far_chip = lax.rem(chip + 2, chips)
    fwd, bwd = fwd_chip * 2 + core, bwd_chip * 2 + core
    peer = chip * 2 + 1 - core

    def load_a(layer, t):
        src = (wg, wu)[t % 2]
        return [pltpu.make_async_copy(src.at[layer, :, pl.ds((t // 2) * TILE, TILE)], wa.at[t], sem_a.at[t])]

    def load_q(layer, t):
        return [pltpu.make_async_copy(wq.at[layer, :, pl.ds(t * TILE, TILE)], wa.at[t], sem_a.at[t])]

    def load_kv(layer):
        t = n_q
        return [
            pltpu.make_async_copy(wk.at[layer], wa.at[t, :, pl.ds(0, head)], sem_a.at[t]),
            pltpu.make_async_copy(wv.at[layer], wa.at[t, :, pl.ds(head, head)], sem_k.at[NKV]),
        ]

    def load_o(layer, t):
        return [pltpu.make_async_copy(wo.at[layer, pl.ds(t * TILE, TILE), :], wb.at[t], sem_b.at[t])]

    def load_d(layer, t):
        return [pltpu.make_async_copy(wd.at[layer, pl.ds(t * TILE, TILE), :], wb.at[t], sem_b.at[t])]

    def begin(copies, priority=1):
        for c in copies:
            c.start(priority=priority)

    def finish(copies):
        for c in copies:
            c.wait()

    def load_cache(g):
        layer = g // (CHUNKS * steps)
        tok = pl.multiple_of(lax.rem(g, CHUNKS * steps) * TOK, TOK)
        slot = lax.rem(g, NKV)
        return [
            pltpu.make_async_copy(kc.at[layer, pl.ds(tok, TOK)], kbuf.at[slot], sem_k.at[slot]),
            pltpu.make_async_copy(vc.at[layer, pl.ds(tok, TOK)], vbuf.at[slot], sem_v.at[slot]),
        ]

    def load_x(ch):
        return [
            pltpu.make_async_copy(x.at[ch], pbuf.at[ch], sem_x.at[ch, 0]),
            pltpu.make_async_copy(x.at[ch, chip, core], hres.at[ch], sem_x.at[ch, 1]),
        ]

    n_attn = n_q + 1

    begin(load_x(0), 0)
    for t in range(n_q):
        begin(load_q(0, t), 0)
    begin(load_kv(0), 0)
    for g in range(NKV):
        begin(load_cache(jnp.int32(g)), 0)
    begin(load_x(1), 0)
    for t in range(n_o):
        begin(load_o(0, t))
    for t in range(n_attn, 2 * n_ff):
        begin(load_a(0, t))
    for t in range(n_o, n_ff):
        begin(load_d(0, t))

    barrier = pltpu.get_barrier_semaphore()
    for other in (peer, fwd, bwd):
        pl.semaphore_signal(barrier, inc=1, device_id={"tp": other}, device_id_type=pl.DeviceIdType.MESH)
    pl.semaphore_wait(barrier, 3)

    def first_norm(ch):
        finish(load_x(ch))

        def body(i, _):
            c, k = i // 2, lax.rem(i, 2)
            h = pbuf[ch, c, k].astype(F32)
            inv = lax.rsqrt(jnp.mean(h * h, axis=-1, keepdims=True) + NORM_EPS)
            cbuf[ch, c, k] = (h * inv * an[0:1, :]).astype(BF)
            return 0

        lax.fori_loop(0, n_tp, body, 0)

    def cols_of(p):
        return pl.ds(p * piece, piece)

    def remote(ch, name, src, dst, target):
        i = COPIES.index(name)
        return pltpu.make_async_remote_copy(
            src_ref=src,
            dst_ref=dst,
            send_sem=ssem.at[ch, i],
            recv_sem=rsem.at[ch, i],
            device_id={"tp": target},
            device_id_type=pl.DeviceIdType.MESH,
        )

    def copy(ch, name):
        if name in ONCE:
            if name == "near":
                return remote(ch, name, ys.at[ch], yr.at[ch], bwd)
            c, target = {
                "g_fwd": (chip, fwd), "g_bwd": (chip, bwd), "g_far": (bwd_chip, fwd),
                "p_own": (chip, peer), "p_bwd": (bwd_chip, peer), "p_fwd": (fwd_chip, peer), "p_far": (far_chip, peer),
            }[name]
            return remote(ch, name, cbuf.at[ch, c, core], cbuf.at[ch, c, core], target)
        p = int(name[-1])
        if name.startswith("part"):
            return remote(ch, name, pbuf.at[ch, :, 1 - core, :, cols_of(p)], dbuf.at[ch, :, :, cols_of(p)], peer)
        if name.startswith("far"):
            return remote(ch, name, xs.at[ch, :, cols_of(p)], xr.at[ch, :, cols_of(p)], fwd)
        return remote(ch, name, zs.at[ch, :, cols_of(p)], zr.at[ch, :, cols_of(p)], fwd)

    def pair(ch, c, cols):
        return pbuf[ch, c, core, :, cols].astype(F32) + dbuf[ch, c, :, cols].astype(F32)

    def exchange(ch, gain, last):
        for p in range(NP):
            copy(ch, f"part{p}").wait_recv()
            xs[ch, :, cols_of(p)] = pair(ch, far_chip, cols_of(p))
            copy(ch, f"far{p}").start()
            yield f"x{p}"
        ys[ch] = pair(ch, bwd_chip, slice(None))
        copy(ch, "near").start()
        yield "near"
        for p in range(NP):
            copy(ch, f"far{p}").wait_recv()
            zs[ch, :, cols_of(p)] = xr[ch, :, cols_of(p)] + pair(ch, fwd_chip, cols_of(p))
            copy(ch, f"relay{p}").start()
            yield f"z{p}"
        copy(ch, "near").wait_recv()
        for p in range(NP):
            copy(ch, f"relay{p}").wait_recv()
        h = (hres[ch].astype(F32) + (pair(ch, chip, slice(None)) + yr[ch] + zr[ch])).astype(BF)
        if last:
            cbuf[ch, chip, core] = h
        else:
            hres[ch] = h
            hf = h.astype(F32)
            inv = lax.rsqrt(jnp.mean(hf * hf, axis=-1, keepdims=True) + NORM_EPS)
            cbuf[ch, chip, core] = (hf * inv * gain[...]).astype(BF)
        for name in ("g_fwd", "g_bwd", "p_own"):
            copy(ch, name).start()
        yield "norm"
        copy(ch, "g_fwd").wait_recv()
        copy(ch, "g_far").start()
        copy(ch, "p_bwd").start()
        copy(ch, "g_bwd").wait_recv()
        copy(ch, "p_fwd").start()
        yield "gather"
        copy(ch, "g_far").wait_recv()
        copy(ch, "p_far").start()
        yield "far"
        for name in ("p_own", "p_bwd", "p_fwd", "p_far"):
            copy(ch, name).wait_recv()
        for name in COPIES:
            copy(ch, name).wait_send()
        yield "end"

    order = (
        [f"x{p}" for p in range(NP)] + ["near"] + [f"z{p}" for p in range(NP)] + ["norm", "gather", "far", "end"]
    )

    def upto(steps_left, name):
        if steps_left is None or name is None:
            return
        gen, at = steps_left
        while at[0] <= order.index(name):
            assert next(gen) == order[at[0]]
            at[0] += 1

    n_col = 512

    def partial(ch, product, own):
        for p in range(NP):
            def body(n, _):
                cols = pl.ds(pl.multiple_of(n * n_col, n_col), n_col)
                pbuf[ch, :, :, :, cols] = product(cols).astype(BF).reshape(chips, 2, rows, n_col)
                return 0

            lax.fori_loop(p * piece // n_col, (p + 1) * piece // n_col, body, 0)
            copy(ch, f"part{p}").start()
            if p >= LAG:
                upto(own, f"x{p - LAG}")

    def normed(ch):
        return cbuf[ch].reshape(chunk, width)

    def attention(layer, ch, own):
        tok = pl.ds(ch * chunk, chunk)
        ct, st = cos[tok, :], sin[tok, :]

        def rope(v):
            return (v * ct + pltpu.roll(v, head // 2, 1) * st).astype(BF).astype(F32)

        for t in range(n_q):
            if ch == 0:
                finish(load_q(layer, t))
            q2 = dot(normed(ch), wa[t])
            for i in range(TILE // head):
                h = t * (TILE // head) + i
                qs[pl.ds(h, chunk, stride=heads), :] = rope(q2[:, i * head:(i + 1) * head])
        if ch == 0:
            finish(load_kv(layer))
        kv = dot(normed(ch), wa[n_q])
        k_new = rope(kv[:, :head])
        v_new = kv[:, head:].astype(BF).astype(F32)
        for h in range(heads):
            kx[pl.ds(h, chunk, stride=heads), :] = k_new
            vx[pl.ds(h, chunk, stride=heads), :] = v_new
        if ch == CHUNKS - 1:
            for t in range(n_attn):
                begin(load_a(layer, t))
        yield "qkv"

        def step(i, _):
            g = (layer * CHUNKS + ch) * steps + i
            slot = lax.rem(g, NKV)
            finish(load_cache(g))
            qrows = GRP * heads
            row_tok = lax.broadcasted_iota(jnp.int32, (qrows, head), 0) // heads
            pos = lax.broadcasted_iota(jnp.int32, (qrows, head), 1)
            for j in range(TOK // GRP):
                r = pl.ds(pl.multiple_of((i * (TOK // GRP) + j) * qrows, qrows), qrows)
                rn = pl.ds(pl.multiple_of(ch * chunk * heads + (i * (TOK // GRP) + j) * qrows, qrows), qrows)
                q = qs[r, :]
                kg = kbuf[slot, pl.ds(j * GRP, GRP)].reshape(GRP * kbuf.shape[2], head)
                vg = vbuf[slot, pl.ds(j * GRP, GRP)].reshape(GRP * kbuf.shape[2], head)
                lg = lax.dot_general(q.astype(BF), kg, (((1,), (1,)), ((), ())), preferred_element_type=F32) * scale
                n = nrow[rn, :]
                parts = [
                    jnp.where(pos < jnp.where(row_tok == b, n, 0), lg[:, b * head:(b + 1) * head], -1e30)
                    for b in range(GRP)
                ]
                l_new = jnp.sum(q * kx[r, :], axis=-1, keepdims=True) * scale
                top = functools.reduce(jnp.maximum, parts)
                m = jnp.maximum(jnp.max(top, axis=-1, keepdims=True), l_new)
                ps = [jnp.exp(b - m) for b in parts]
                p_new = jnp.exp(l_new - m)
                total = jnp.sum(functools.reduce(jnp.add, ps), axis=-1, keepdims=True) + p_new
                o = dot(jnp.concatenate(ps, axis=1).astype(BF), vg)
                o = o + p_new.astype(BF).astype(F32) * vx[r, :]
                osc[r, :] = o / total

            @pl.when(g + NKV < n_layers * CHUNKS * steps)
            def _():
                begin(load_cache(g + NKV), 0)

            return 0

        for lo, hi in ((0, steps // 2), (steps // 2, steps)):
            lax.fori_loop(lo, hi, step, 0)
            yield lo

        for h in range(heads):
            obf[:, h * head:(h + 1) * head] = osc[pl.ds(h, chunk, stride=heads), :].astype(BF)
        if ch == 0:
            for t in range(n_o):
                finish(load_o(layer, t))

        def product(cols):
            return functools.reduce(
                jnp.add, [dot(obf[:, t * TILE:(t + 1) * TILE], wb[t, :, cols]) for t in range(n_o)]
            )

        partial(ch, product, own)
        if ch == CHUNKS - 1:
            for t in range(n_o):
                begin(load_d(layer, t))

    def mlp(layer, ch, own):
        more = ch == CHUNKS - 1 and layer + 1 < n_layers

        def gate_up(j, _):
            if ch == 0:
                for t, src in enumerate((wg, wu)):
                    pltpu.make_async_copy(src.at[layer, :, pl.ds(0, TILE)], wa.at[2 * j + t], sem_a.at[2 * j + t]).wait()
            gate = dot(normed(ch), wa[2 * j])
            up = dot(normed(ch), wa[2 * j + 1])
            act[j] = (gate * (1.0 / (1.0 + jnp.exp(-gate))) * up).astype(BF)
            return 0

        for lo, hi in ((0, 3), (3, 5), (5, n_ff)):
            lax.fori_loop(lo, hi, gate_up, 0)
            if more:
                for t in range(2 * lo, 2 * hi):
                    if t < n_q:
                        begin(load_q(layer + 1, t))
                    elif t == n_q:
                        begin(load_kv(layer + 1))
                    else:
                        begin(load_a(layer + 1, t))
            yield lo
        if ch == 0:
            for t in range(n_ff):
                finish(load_d(layer, t))

        def product(cols):
            return functools.reduce(jnp.add, [dot(act[t], wb[t, :, cols]) for t in range(n_ff)])

        partial(ch, product, own)
        if more:
            for t in range(n_ff):
                begin(load_o(layer + 1, t) if t < n_o else load_d(layer + 1, t))

    stages = [(kind, layer, ch) for layer in range(n_layers) for kind in ("attn", "mlp") for ch in range(CHUNKS)]
    other = None
    for kind, layer, ch in stages:
        last = kind == "mlp" and layer + 1 == n_layers
        gain = mn.at[layer:layer + 1] if kind == "attn" else an.at[(layer + 1) % n_layers:(layer + 1) % n_layers + 1]
        own = (exchange(ch, gain, last), [0])
        if kind == "attn":
            if layer == 0:
                first_norm(ch)
            for done in attention(layer, ch, own):
                upto(other, {"qkv": f"z{NP - 1}", 0: None}.get(done, "norm"))
        else:
            for done in mlp(layer, ch, own):
                upto(other, {0: f"z{NP - 1}", 3: "norm"}.get(done, "norm"))
        for p in range(NP - LAG, NP):
            upto(own, f"x{p}")
        upto(own, "near")
        upto(other, "gather")
        upto(own, "z0")
        upto(other, "far")
        upto(own, "z1")
        upto(other, "end")
        other = own
    upto(other, "end")
    outs = [pltpu.make_async_copy(cbuf.at[ch], out.at[ch], sem_x.at[ch, 0]) for ch in range(CHUNKS)]
    begin(outs)
    finish(outs)


def solution(mesh):
    cache_spec = P(None, "dp", None, "tp", None)
    col_spec = P(None, None, "tp")
    row_spec = P(None, "tp", None)
    in_specs = (P("dp", None), P("dp"), cache_spec, cache_spec, P(), P(), col_spec, col_spec, col_spec, row_spec, col_spec, col_spec, row_spec)

    def local_layers(x, lengths, k_cache, v_cache, attn_norm, mlp_norm, w_q, w_k, w_v, w_o, w_gate, w_up, w_down):
        batch, width = x.shape
        layers, _, seq, _, head = k_cache.shape
        heads = w_q.shape[2] // head
        inner = w_o.shape[1]
        ff = w_gate.shape[2]
        n_tp = mesh.shape["tp"]
        chunk = batch // CHUNKS
        rows = chunk // n_tp
        split = (n_tp // 2, 2, rows, width)

        inv_freq = ROPE_BASE ** (-jnp.arange(0, head, 2).astype(F32) / head)
        angles = lengths.astype(F32)[:, None] * inv_freq[None, :]
        ct, st = jnp.cos(angles), jnp.sin(angles)
        cos = jnp.concatenate([ct, ct], axis=1)
        sin = jnp.concatenate([-st, st], axis=1)
        nrow = jnp.broadcast_to(lengths[:, None, None], (batch, heads, head)).reshape(batch * heads, head)

        vmem = pl.BlockSpec(memory_space=pltpu.VMEM)
        hbm = pl.BlockSpec(memory_space=pl.ANY)
        n_wa = 2 * (ff // TILE)
        n_wb = ff // TILE
        f32_rows = pltpu.VMEM((CHUNKS, rows, width), F32)
        y = pl.pallas_call(
            kernel,
            out_shape=jax.ShapeDtypeStruct((CHUNKS, *split), BF),
            in_specs=[hbm, vmem, vmem, vmem, hbm, hbm, vmem, vmem] + [hbm] * 7,
            out_specs=hbm,
            scratch_shapes=[
                pltpu.VMEM((n_wa, width, TILE), BF),
                pltpu.VMEM((n_wb, TILE, width), BF),
                pltpu.VMEM((NKV, TOK, seq, head), BF),
                pltpu.VMEM((NKV, TOK, seq, head), BF),
                pltpu.VMEM((CHUNKS, *split), BF),
                pltpu.VMEM((CHUNKS, *split), BF),
                pltpu.VMEM((CHUNKS, n_tp // 2, rows, width), BF),
                f32_rows, f32_rows, f32_rows, f32_rows, f32_rows, f32_rows,
                pltpu.VMEM((CHUNKS, rows, width), BF),
                pltpu.VMEM((n_wb, chunk, TILE), BF),
                pltpu.VMEM((chunk * heads, head), F32),
                pltpu.VMEM((chunk * heads, head), F32),
                pltpu.VMEM((chunk * heads, head), F32),
                pltpu.VMEM((chunk * heads, head), F32),
                pltpu.VMEM((chunk, inner), BF),
                pltpu.SemaphoreType.DMA((n_wa,)),
                pltpu.SemaphoreType.DMA((n_wb,)),
                pltpu.SemaphoreType.DMA((NKV + 1,)),
                pltpu.SemaphoreType.DMA((NKV,)),
                pltpu.SemaphoreType.DMA((CHUNKS, 2)),
                pltpu.SemaphoreType.DMA((CHUNKS, len(COPIES))),
                pltpu.SemaphoreType.DMA((CHUNKS, len(COPIES))),
            ],
            compiler_params=pltpu.CompilerParams(
                collective_id=0, has_side_effects=True, vmem_limit_bytes=67043328
            ),
            name="decoder",
        )(
            x.reshape(CHUNKS, *split), cos, sin, nrow,
            k_cache.reshape(layers, batch, seq, head), v_cache.reshape(layers, batch, seq, head),
            attn_norm, mlp_norm, w_q, w_k, w_v, w_o, w_gate, w_up, w_down,
        )
        return y.reshape(batch, width)

    return jax.shard_map(local_layers, mesh=mesh, in_specs=in_specs, out_specs=P("dp", None), check_vma=False)
```

time: 240 us -> 208 us (0.87)
  Pallas kernels: 233 us -> 200 us
    pallas_call x1, Pallas kernels: 233 us -> 200 us  [local_layers(): pl.pallas_call(kernel, out_shape=jax.ShapeDtypeStruct((CHUNKS, *split), B...]
where the time goes in v1:
time: 208 us
  Pallas kernels  200 us (96%)
  local copies, waits for them, and re-layouts  5.01 us (2%)
  other arithmetic  2.1 us (1%)
    pallas_call x1, Pallas kernels, local_layers(): pl.pallas_call(kernel, out_shape=jax.ShapeDtypeStruct((CHUNKS, *split), B...  200 us

profile of v1, /device:TPU:113, one launch (start us, length us, event | category | flops | bytes accessed | tf_op | source)
XLA Modules:
  0.0 207.5 jit_solution(5427365236407919317)
XLA Ops:
  0.0 0.7 convert_element_type.10
  0.7 0.8 broadcast_in_dim.12
  1.5 0.1 broadcast_in_dim.13
  1.6 0.5 fusion
  2.1 0.9 pad_maximum_fusion
  3.0 1.0 broadcast_in_dim.14.nrow
  4.0 200.4 %decoder.1 = bf16[2,4,2,16,4096]{4,3,2,1,0:T(8,128)(2,1)} custom-call(bf16[2,4,2,16,4096]{4,3,2,1,0:T(8,128)(2,1)} %bitcast.7, f32[256,128]{1,0:T(8,128)} %get-tuple-element.8.cos, f32[256,128]{1,0:T(8,128)} %get-tuple-element.9.sin, s32[1024,128]{1,0:T(8,128)} %broadcast_in_dim.14.nrow, bf16[2,256,128,128]{3,2,1,0:T(8,128)(2,1)} %bitcast.4, ...), custom_call_target="tpu_custom_call" | custom-call | tf_op jit(solution)/shard_map/decoder/pallas_call | solution.py:415
  204.4 3.1 %copy.15 = bf16[256,4096]{1,0:T(8,128)(2,1)} copy(bf16[256,4096]{1,0:T(8,128)(2,1)} %bitcast.6) | data formatting | bytes 4194304
  (1 shorter events, 0.0 us)

commit v2 on v1

--- a/solution.py
+++ b/solution.py
@@ -14,10 +14,31 @@
 CHUNKS = 2
 TOK = 16
 NKV = 4
+PAIR = 2
 GRP = 4
 TILE = 256
 NP = 4
-LAG = 2
+H_CUT = (0, 3, 4)
+G_CUT = (0, 1, 6, 7)
+PLAN = {'attn': {'q0': ('o:z2',),
+          'q1': ('o:z3',),
+          'h3': ('o:norm',),
+          'h4': ('o:spread',),
+          'p2': ('x0',),
+          'p3': ('x1', 'o:gather'),
+          'done': ('x2', 'x3', 'near', 'z0', 'o:far', 'z1', 'o:end')},
+ 'mlp': {'g1': ('o:z2', 'o:z3'),
+         'g6': ('o:norm',),
+         'g7': ('o:spread',),
+         'p2': ('x0',),
+         'p3': ('x1', 'o:gather'),
+         'done': ('x2', 'x3', 'near', 'z0', 'o:far', 'z1', 'o:end')},
+ 'last': {'g1': ('o:z2', 'o:z3'),
+          'g6': ('o:norm',),
+          'g7': ('o:spread',),
+          'p2': ('x0',),
+          'p3': ('x1', 'o:gather'),
+          'done': ('x2', 'x3', 'near', 'z0', 'z1', 'z2', 'o:far', 'z3', 'o:end')}}
 ONCE = ("near", "g_fwd", "g_bwd", "g_far", "p_own", "p_bwd", "p_fwd", "p_far")
 COPIES = ONCE + tuple(f"{k}{p}" for k in ("part", "far", "relay") for p in range(NP))
 
@@ -27,8 +48,8 @@
 
 
 def kernel(
-    x, cos, sin, nrow, kc, vc, an, mn, wq, wk, wv, wo, wg, wu, wd, out,
-    wa, wb, kbuf, vbuf, cbuf, pbuf, dbuf, xs, ys, zs, xr, yr, zr, hres, act, qs, kx, vx, osc, obf,
+    x, lengths, freq, kc, vc, an, mn, wq, wk, wv, wo, wg, wu, wd, out,
+    wa, wb, kbuf, vbuf, cbuf, pbuf, dbuf, xs, ys, zs, xr, yr, zr, hres, act, qs, kx, vx, osc, obf, cos, sin, nrow,
     sem_a, sem_b, sem_k, sem_v, sem_x, ssem, rsem,
 ):
     n_layers = wq.shape[0]
@@ -105,23 +126,37 @@
     for t in range(n_q):
         begin(load_q(0, t), 0)
     begin(load_kv(0), 0)
-    for g in range(NKV):
-        begin(load_cache(jnp.int32(g)), 0)
-    begin(load_x(1), 0)
-    for t in range(n_o):
-        begin(load_o(0, t))
-    for t in range(n_attn, 2 * n_ff):
-        begin(load_a(0, t))
-    for t in range(n_o, n_ff):
-        begin(load_d(0, t))
+
+    def load_rest():
+        for g in range(NKV):
+            begin(load_cache(jnp.int32(g)), 0)
+        begin(load_x(1), 0)
+        for t in range(n_o):
+            begin(load_o(0, t))
+        for t in range(n_attn, 2 * n_ff):
+            begin(load_a(0, t))
+        for t in range(n_o, n_ff):
+            begin(load_d(0, t))
 
     barrier = pltpu.get_barrier_semaphore()
     for other in (peer, fwd, bwd):
         pl.semaphore_signal(barrier, inc=1, device_id={"tp": other}, device_id_type=pl.DeviceIdType.MESH)
-    pl.semaphore_wait(barrier, 3)
+
+    def tables(ch):
+        n = jnp.broadcast_to(lengths[ch:ch + 1, :].astype(F32), (chunk, chunk)).T
+        tok = pl.ds(ch * chunk, chunk)
+        angles = n[:, :head] * freq[...]
+        turn = jnp.sin(angles)
+        cos[tok, :] = jnp.cos(angles)
+        sin[tok, :] = jnp.where(lax.broadcasted_iota(jnp.int32, (chunk, head), 1) < head // 2, -turn, turn)
+        for h in range(heads):
+            nrow[pl.ds(ch * chunk * heads + h, chunk, stride=heads), :] = n[:, :head].astype(jnp.int32)
 
     def first_norm(ch):
+        tables(ch)
         finish(load_x(ch))
+        if ch == 0:
+            load_rest()
 
         def body(i, _):
             c, k = i // 2, lax.rem(i, 2)
@@ -190,15 +225,18 @@
             hf = h.astype(F32)
             inv = lax.rsqrt(jnp.mean(hf * hf, axis=-1, keepdims=True) + NORM_EPS)
             cbuf[ch, chip, core] = (hf * inv * gain[...]).astype(BF)
-        for name in ("g_fwd", "g_bwd", "p_own"):
+        for name in ("g_fwd", "p_own"):
             copy(ch, name).start()
         yield "norm"
+        copy(ch, "g_bwd").start()
+        yield "spread"
         copy(ch, "g_fwd").wait_recv()
         copy(ch, "g_far").start()
         copy(ch, "p_bwd").start()
+        yield "gather"
         copy(ch, "g_bwd").wait_recv()
         copy(ch, "p_fwd").start()
-        yield "gather"
+        yield "back"
         copy(ch, "g_far").wait_recv()
         copy(ch, "p_far").start()
         yield "far"
@@ -209,7 +247,7 @@
         yield "end"
 
     order = (
-        [f"x{p}" for p in range(NP)] + ["near"] + [f"z{p}" for p in range(NP)] + ["norm", "gather", "far", "end"]
+        [f"x{p}" for p in range(NP)] + ["near"] + [f"z{p}" for p in range(NP)] + ["norm", "spread", "gather", "back", "far", "end"]
     )
 
     def upto(steps_left, name):
@@ -217,27 +255,28 @@
             return
         gen, at = steps_left
         while at[0] <= order.index(name):
-            assert next(gen) == order[at[0]]
+            with jax.named_scope(f"{order[at[0]]}"):
+                assert next(gen) == order[at[0]]
             at[0] += 1
 
-    n_col = 512
-
-    def partial(ch, product, own):
+    n_col = 1024
+
+    def partial(ch, product):
         for p in range(NP):
             def body(n, _):
                 cols = pl.ds(pl.multiple_of(n * n_col, n_col), n_col)
                 pbuf[ch, :, :, :, cols] = product(cols).astype(BF).reshape(chips, 2, rows, n_col)
                 return 0
 
-            lax.fori_loop(p * piece // n_col, (p + 1) * piece // n_col, body, 0)
+            with jax.named_scope("partial"):
+                lax.fori_loop(p * piece // n_col, (p + 1) * piece // n_col, body, 0)
             copy(ch, f"part{p}").start()
-            if p >= LAG:
-                upto(own, f"x{p - LAG}")
+            yield f"p{p}"
 
     def normed(ch):
         return cbuf[ch].reshape(chunk, width)
 
-    def attention(layer, ch, own):
+    def attention(layer, ch):
         tok = pl.ds(ch * chunk, chunk)
         ct, st = cos[tok, :], sin[tok, :]
 
@@ -251,6 +290,7 @@
             for i in range(TILE // head):
                 h = t * (TILE // head) + i
                 qs[pl.ds(h, chunk, stride=heads), :] = rope(q2[:, i * head:(i + 1) * head])
+            yield f"q{t}"
         if ch == 0:
             finish(load_kv(layer))
         kv = dot(normed(ch), wa[n_q])
@@ -264,45 +304,59 @@
                 begin(load_a(layer, t))
         yield "qkv"
 
+        seq = kbuf.shape[2]
+        qrows = GRP * heads
+
         def step(i, _):
-            g = (layer * CHUNKS + ch) * steps + i
-            slot = lax.rem(g, NKV)
-            finish(load_cache(g))
-            qrows = GRP * heads
+            first = (layer * CHUNKS + ch) * steps + i * PAIR
+            for b in range(PAIR):
+                finish(load_cache(first + b))
             row_tok = lax.broadcasted_iota(jnp.int32, (qrows, head), 0) // heads
             pos = lax.broadcasted_iota(jnp.int32, (qrows, head), 1)
-            for j in range(TOK // GRP):
-                r = pl.ds(pl.multiple_of((i * (TOK // GRP) + j) * qrows, qrows), qrows)
-                rn = pl.ds(pl.multiple_of(ch * chunk * heads + (i * (TOK // GRP) + j) * qrows, qrows), qrows)
-                q = qs[r, :]
-                kg = kbuf[slot, pl.ds(j * GRP, GRP)].reshape(GRP * kbuf.shape[2], head)
-                vg = vbuf[slot, pl.ds(j * GRP, GRP)].reshape(GRP * kbuf.shape[2], head)
-                lg = lax.dot_general(q.astype(BF), kg, (((1,), (1,)), ((), ())), preferred_element_type=F32) * scale
-                n = nrow[rn, :]
+            groups = [(b, j) for b in range(PAIR) for j in range(TOK // GRP)]
+
+            def at(n, base=0):
+                return pl.ds(pl.multiple_of(base + (i * len(groups) + n) * qrows, qrows), qrows)
+
+            logits, probs = [], []
+            for n, (b, j) in enumerate(groups):
+                kg = kbuf[lax.rem(first + b, NKV), pl.ds(j * GRP, GRP)].reshape(GRP * seq, head)
+                q = qs[at(n), :].astype(BF)
+                logits.append(lax.dot_general(q, kg, (((1,), (1,)), ((), ())), preferred_element_type=F32) * scale)
+            for n, lg in enumerate(logits):
+                limit = nrow[at(n, ch * chunk * heads), :]
                 parts = [
-                    jnp.where(pos < jnp.where(row_tok == b, n, 0), lg[:, b * head:(b + 1) * head], -1e30)
-                    for b in range(GRP)
+                    jnp.where(pos < jnp.where(row_tok == t, limit, 0), lg[:, t * seq:(t + 1) * seq], -1e30)
+                    for t in range(GRP)
                 ]
-                l_new = jnp.sum(q * kx[r, :], axis=-1, keepdims=True) * scale
-                top = functools.reduce(jnp.maximum, parts)
-                m = jnp.maximum(jnp.max(top, axis=-1, keepdims=True), l_new)
-                ps = [jnp.exp(b - m) for b in parts]
+                l_new = jnp.sum(qs[at(n), :] * kx[at(n), :], axis=-1, keepdims=True) * scale
+                m = jnp.maximum(jnp.max(functools.reduce(jnp.maximum, parts), axis=-1, keepdims=True), l_new)
+                ps = [jnp.exp(t - m) for t in parts]
                 p_new = jnp.exp(l_new - m)
                 total = jnp.sum(functools.reduce(jnp.add, ps), axis=-1, keepdims=True) + p_new
-                o = dot(jnp.concatenate(ps, axis=1).astype(BF), vg)
-                o = o + p_new.astype(BF).astype(F32) * vx[r, :]
-                osc[r, :] = o / total
-
-            @pl.when(g + NKV < n_layers * CHUNKS * steps)
-            def _():
-                begin(load_cache(g + NKV), 0)
+                probs.append((jnp.concatenate(ps, axis=1).astype(BF), p_new, total))
+            for n, (b, j) in enumerate(groups):
+                p, p_new, total = probs[n]
+                vg = vbuf[lax.rem(first + b, NKV), pl.ds(j * GRP, GRP)].reshape(GRP * seq, head)
+                o = dot(p, vg) + p_new.astype(BF).astype(F32) * vx[at(n), :]
+                osc[at(n), :] = o / total
+
+            for b in range(PAIR):
+                g = first + b
+
+                @pl.when(g + NKV < n_layers * CHUNKS * steps)
+                def _():
+                    begin(load_cache(g + NKV), 0)
 
             return 0
 
-        for lo, hi in ((0, steps // 2), (steps // 2, steps)):
-            lax.fori_loop(lo, hi, step, 0)
-            yield lo
-
+        for lo, hi in zip(H_CUT, H_CUT[1:]):
+            with jax.named_scope("heads"):
+                lax.fori_loop(lo, hi, step, 0)
+            yield f"h{hi}"
+
+        if layer == 0 and ch == 0:
+            pl.semaphore_wait(barrier, 3)
         for h in range(heads):
             obf[:, h * head:(h + 1) * head] = osc[pl.ds(h, chunk, stride=heads), :].astype(BF)
         if ch == 0:
@@ -314,12 +368,12 @@
                 jnp.add, [dot(obf[:, t * TILE:(t + 1) * TILE], wb[t, :, cols]) for t in range(n_o)]
             )
 
-        partial(ch, product, own)
+        yield from partial(ch, product)
         if ch == CHUNKS - 1:
             for t in range(n_o):
                 begin(load_d(layer, t))
 
-    def mlp(layer, ch, own):
+    def mlp(layer, ch):
         more = ch == CHUNKS - 1 and layer + 1 < n_layers
 
         def gate_up(j, _):
@@ -331,8 +385,9 @@
             act[j] = (gate * (1.0 / (1.0 + jnp.exp(-gate))) * up).astype(BF)
             return 0
 
-        for lo, hi in ((0, 3), (3, 5), (5, n_ff)):
-            lax.fori_loop(lo, hi, gate_up, 0)
+        for lo, hi in zip(G_CUT, G_CUT[1:]):
+            with jax.named_scope("gateup"):
+                lax.fori_loop(lo, hi, gate_up, 0)
             if more:
                 for t in range(2 * lo, 2 * hi):
                     if t < n_q:
@@ -341,7 +396,7 @@
                         begin(load_kv(layer + 1))
                     else:
                         begin(load_a(layer + 1, t))
-            yield lo
+            yield f"g{hi}"
         if ch == 0:
             for t in range(n_ff):
                 finish(load_d(layer, t))
@@ -349,7 +404,7 @@
         def product(cols):
             return functools.reduce(jnp.add, [dot(act[t], wb[t, :, cols]) for t in range(n_ff)])
 
-        partial(ch, product, own)
+        yield from partial(ch, product)
         if more:
             for t in range(n_ff):
                 begin(load_o(layer + 1, t) if t < n_o else load_d(layer + 1, t))
@@ -357,25 +412,21 @@
     stages = [(kind, layer, ch) for layer in range(n_layers) for kind in ("attn", "mlp") for ch in range(CHUNKS)]
     other = None
     for kind, layer, ch in stages:
+        tags = attention(layer, ch) if kind == "attn" else mlp(layer, ch)
         last = kind == "mlp" and layer + 1 == n_layers
         gain = mn.at[layer:layer + 1] if kind == "attn" else an.at[(layer + 1) % n_layers:(layer + 1) % n_layers + 1]
         own = (exchange(ch, gain, last), [0])
-        if kind == "attn":
-            if layer == 0:
-                first_norm(ch)
-            for done in attention(layer, ch, own):
-                upto(other, {"qkv": f"z{NP - 1}", 0: None}.get(done, "norm"))
-        else:
-            for done in mlp(layer, ch, own):
-                upto(other, {0: f"z{NP - 1}", 3: "norm"}.get(done, "norm"))
-        for p in range(NP - LAG, NP):
-            upto(own, f"x{p}")
-        upto(own, "near")
-        upto(other, "gather")
-        upto(own, "z0")
-        upto(other, "far")
-        upto(own, "z1")
-        upto(other, "end")
+        plan = PLAN["last" if last and ch == CHUNKS - 1 else kind]
+
+        def run(tag):
+            for step in plan.get(tag, ()):
+                upto(other if step.startswith("o:") else own, step.removeprefix("o:"))
+
+        if kind == "attn" and layer == 0:
+            first_norm(ch)
+        for tag in tags:
+            run(tag)
+        run("done")
         other = own
     upto(other, "end")
     outs = [pltpu.make_async_copy(cbuf.at[ch], out.at[ch], sem_x.at[ch, 0]) for ch in range(CHUNKS)]
@@ -400,12 +451,8 @@
         rows = chunk // n_tp
         split = (n_tp // 2, 2, rows, width)
 
-        inv_freq = ROPE_BASE ** (-jnp.arange(0, head, 2).astype(F32) / head)
-        angles = lengths.astype(F32)[:, None] * inv_freq[None, :]
-        ct, st = jnp.cos(angles), jnp.sin(angles)
-        cos = jnp.concatenate([ct, ct], axis=1)
-        sin = jnp.concatenate([-st, st], axis=1)
-        nrow = jnp.broadcast_to(lengths[:, None, None], (batch, heads, head)).reshape(batch * heads, head)
+        freq = ROPE_BASE ** (-jnp.arange(0, head, 2).astype(F32) / head)
+        freq = jnp.concatenate([freq, freq])[None, :]
 
         vmem = pl.BlockSpec(memory_space=pltpu.VMEM)
         hbm = pl.BlockSpec(memory_space=pl.ANY)
@@ -415,7 +462,7 @@
         y = pl.pallas_call(
             kernel,
             out_shape=jax.ShapeDtypeStruct((CHUNKS, *split), BF),
-            in_specs=[hbm, vmem, vmem, vmem, hbm, hbm, vmem, vmem] + [hbm] * 7,
+            in_specs=[hbm, vmem, vmem, hbm, hbm, vmem, vmem] + [hbm] * 7,
             out_specs=hbm,
             scratch_shapes=[
                 pltpu.VMEM((n_wa, width, TILE), BF),
@@ -433,6 +480,9 @@
                 pltpu.VMEM((chunk * heads, head), F32),
                 pltpu.VMEM((chunk * heads, head), F32),
                 pltpu.VMEM((chunk, inner), BF),
+                pltpu.VMEM((batch, head), F32),
+                pltpu.VMEM((batch, head), F32),
+                pltpu.VMEM((batch * heads, head), jnp.int32),
                 pltpu.SemaphoreType.DMA((n_wa,)),
                 pltpu.SemaphoreType.DMA((n_wb,)),
                 pltpu.SemaphoreType.DMA((NKV + 1,)),
@@ -446,7 +496,7 @@
             ),
             name="decoder",
         )(
-            x.reshape(CHUNKS, *split), cos, sin, nrow,
+            x.reshape(CHUNKS, *split), lengths.reshape(CHUNKS, chunk), freq,
             k_cache.reshape(layers, batch, seq, head), v_cache.reshape(layers, batch, seq, head),
             attn_norm, mlp_norm, w_q, w_k, w_v, w_o, w_gate, w_up, w_down,
         )

time: 208 us -> 160 us (0.77)
  Pallas kernels: 200 us -> 156 us
    pallas_call x1, Pallas kernels: 200 us -> 156 us  [local_layers(): pl.pallas_call(kernel, out_shape=jax.ShapeDtypeStruct((CHUNKS, *split), B...]
where the time goes in v2:
time: 160 us
  Pallas kernels  156 us (98%)
  local copies, waits for them, and re-layouts  3.13 us (2%)
    pallas_call x1, Pallas kernels, local_layers(): pl.pallas_call(kernel, out_shape=jax.ShapeDtypeStruct((CHUNKS, *split), B...  156 us

profile of v2, /device:TPU:113, one launch (start us, length us, event | category | flops | bytes accessed | tf_op | source)
XLA Modules:
  0.0 159.9 jit_solution(13870645196733558739)
XLA Ops:
  0.0 0.6 maximum_bitcast_fusion.freq
  0.6 156.2 %decoder.1 = bf16[2,4,2,16,4096]{4,3,2,1,0:T(8,128)(2,1)} custom-call(bf16[2,4,2,16,4096]{4,3,2,1,0:T(8,128)(2,1)} %bitcast.10, s32[2,128]{1,0:T(2,128)} %bitcast.11, f32[1,128]{1,0:T(1,128)} %maximum_bitcast_fusion.freq, bf16[2,256,128,128]{3,2,1,0:T(8,128)(2,1)} %bitcast.7, bf16[2,256,128,128]{3,2,1,0:T(8,128)(2,1)} %bitcast.8, f32[2,4096]{1,0:T(2,128)} %an.1, ...), custom_call_target="tpu_custom_call" | custom-call | tf_op jit(solution)/shard_map/decoder/pallas_call | solution.py:462
  156.8 3.1 %copy.15 = bf16[256,4096]{1,0:T(8,128)(2,1)} copy(bf16[256,4096]{1,0:T(8,128)(2,1)} %bitcast.9) | data formatting | bytes 4194304
  (1 shorter events, 0.0 us)

commit v3 on v2

--- a/solution.py
+++ b/solution.py
@@ -22,23 +22,20 @@
 G_CUT = (0, 1, 6, 7)
 PLAN = {'attn': {'q0': ('o:z2',),
           'q1': ('o:z3',),
-          'h3': ('o:norm',),
-          'h4': ('o:spread',),
+          'h3': ('o:norm', 'o:spread'),
           'p2': ('x0',),
           'p3': ('x1', 'o:gather'),
           'done': ('x2', 'x3', 'near', 'z0', 'o:far', 'z1', 'o:end')},
  'mlp': {'g1': ('o:z2', 'o:z3'),
-         'g6': ('o:norm',),
-         'g7': ('o:spread',),
+         'g6': ('o:norm', 'o:spread'),
          'p2': ('x0',),
          'p3': ('x1', 'o:gather'),
          'done': ('x2', 'x3', 'near', 'z0', 'o:far', 'z1', 'o:end')},
  'last': {'g1': ('o:z2', 'o:z3'),
-          'g6': ('o:norm',),
-          'g7': ('o:spread',),
+          'g6': ('o:norm', 'o:spread'),
           'p2': ('x0',),
           'p3': ('x1', 'o:gather'),
-          'done': ('x2', 'x3', 'near', 'z0', 'z1', 'z2', 'o:far', 'z3', 'o:end')}}
+          'done': ('x2', 'x3', 'near', 'z0', 'z1', 'z2', 'z3', 'o:far', 'o:end')}}
 ONCE = ("near", "g_fwd", "g_bwd", "g_far", "p_own", "p_bwd", "p_fwd", "p_far")
 COPIES = ONCE + tuple(f"{k}{p}" for k in ("part", "far", "relay") for p in range(NP))
 

time: 160 us -> 159 us (level)
  no operation moved by 1% of the time
where the time goes in v3:
time: 159 us
  Pallas kernels  155 us (97%)
  local copies, waits for them, and re-layouts  3.13 us (2%)
    pallas_call x1, Pallas kernels, local_layers(): pl.pallas_call(kernel, out_shape=jax.ShapeDtypeStruct((CHUNKS, *split), B...  155 us

profile of v3, /device:TPU:113, one launch (start us, length us, event | category | flops | bytes accessed | tf_op | source)
XLA Modules:
  0.0 159.0 jit_solution(4797715589102080127)
XLA Ops:
  0.0 0.6 maximum_bitcast_fusion.freq
  0.6 155.3 %decoder.1 = bf16[2,4,2,16,4096]{4,3,2,1,0:T(8,128)(2,1)} custom-call(bf16[2,4,2,16,4096]{4,3,2,1,0:T(8,128)(2,1)} %bitcast.10, s32[2,128]{1,0:T(2,128)} %bitcast.11, f32[1,128]{1,0:T(1,128)} %maximum_bitcast_fusion.freq, bf16[2,256,128,128]{3,2,1,0:T(8,128)(2,1)} %bitcast.7, bf16[2,256,128,128]{3,2,1,0:T(8,128)(2,1)} %bitcast.8, f32[2,4096]{1,0:T(2,128)} %an.1, ...), custom_call_target="tpu_custom_call" | custom-call | tf_op jit(solution)/shard_map/decoder/pallas_call | solution.py:459
  155.9 3.1 %copy.15 = bf16[256,4096]{1,0:T(8,128)(2,1)} copy(bf16[256,4096]{1,0:T(8,128)(2,1)} %bitcast.9) | data formatting | bytes 4194304
  (1 shorter events, 0.0 us)
